TPU v7x, 256 devices: a whole 4x4x8 slice. The times are simulated.
256 devices in a mesh: slab: 32 (over z, x_hi, core), ang: 8 (over x_lo, y).
Axes of the slice: x: 4 (x_hi: 2, x_lo: 2; x = x_hi * 2 + x_lo), y: 4, z: 8, core: 2. Of those that a mesh axis runs over, the one named last changes fastest.
Arguments:
- volume: float32 [256, 256, 4096], P('slab', 'ang'), may hold values from 0.1 to 3
- measured: bfloat16 [8, 1024, 4096], P('ang', 'slab'), may hold values from 0 to 2
- foot_start: int32 [32, 8], P('slab', 'ang'), may hold values from 0 to 992, as said below
- foot_len: int32 [32, 8], P('slab', 'ang'), may hold values from 32 to 96
- order: int32 [64], replicated, may hold values from 0 to 63, each once
- ray_table: float32 [64, 256], replicated, may hold values from 0.001953125 to 0.0078125
Outputs:
- updated: float32 [256, 256, 4096], P('slab', 'ang')
- residual: float32 [8, 1024, 4096], P('ang', 'slab')
Inputs may be any that keep to these rules, and one draw needn't show every extreme that they name: foot_start[s, j] + foot_len[s, j] <= 1024; the footprint of slab s lies within rows (s - 2) * 32 to (s + 3) * 32.
All inputs are finite; a program needn't handle non-finite values.
Results may differ from a plain program's by a relative error of at most 0.0003.
Values sent between devices are 32-bit elements; how exact they have to be, the bound alone decides.
A program may use at most 64 MiB of HBM per device.

v0:
```python
import math

import jax
import jax.numpy as jnp
from jax import lax
from jax.sharding import PartitionSpec as P

ZDEV = 8
ANGLES = 8


def from_behind(value, axis, steps):
    count = lax.axis_size(axis)
    leading, last = (max(0, -steps), min(count, count - steps))
    return lax.ppermute(value, axis, [(source, source + steps) for source in range(leading, last)])


def with_halo(value, sides, width):
    for axis, dim in sides:
        devices, length = (lax.axis_size(axis), value.shape[dim])
        up = [(i, (i + 1) % devices) for i in range(devices - 1)]
        down = [(j, i) for i, j in up]
        last = lax.slice_in_dim(value, length - width, length, axis=dim)
        leading = lax.slice_in_dim(value, 0, width, axis=dim)
        before = lax.ppermute(last, axis, up)
        after = lax.ppermute(leading, axis, down)
        value = jnp.concatenate([before, value, after], axis=dim)
    return value


def in_blocks(value, dim, devices):
    before, after = (value.shape[:dim], value.shape[dim + 1 :])
    return jnp.moveaxis(value.reshape(*before, devices, -1, *after), dim, 0)


def summed_on_arrival(value, axis, dim):
    tiles = in_blocks(value, dim, lax.axis_size(axis))
    arrived = lax.all_to_all(tiles, axis, split_axis=0, concat_axis=0, tiled=True)
    return arrived.sum(axis=0)


def joined_along(tiles, dim):
    lengths = list(tiles.shape[1:])
    lengths[dim] *= tiles.shape[0]
    return jnp.moveaxis(tiles, 0, dim).reshape(lengths)


def copy_for_each(value, axis):
    devices = lax.axis_size(axis)
    return lax.all_to_all(
        jnp.broadcast_to(value[None], (devices, *value.shape)), axis, 0, 0, tiled=True
    )


def gather_directly(value, axis, dim):
    return joined_along(copy_for_each(value, axis), dim)


def side_by_side(arrays, axis, dim, along):
    widths = [math.prod(a.shape[along:]) for a in arrays]
    both = jnp.concatenate(
        [a.reshape(*a.shape[:along], w) for a, w in zip(arrays, widths)], axis=along
    )
    filled = gather_directly(both, axis, dim)
    tiles = jnp.split(filled, [sum(widths[:k]) for k in range(1, len(widths))], axis=along)
    return tuple(
        (b.reshape(*filled.shape[:along], *a.shape[along:]) for a, b in zip(arrays, tiles))
    )


def hat_weights(starts, lengths, rows):
    first = starts[..., None, None]
    span_len = lengths[..., None, None]
    span = span_len / ZDEV
    centre = first + (jnp.arange(ZDEV, dtype=jnp.float32)[None, :] + 0.5) * span
    row_pos = rows[:, None]
    weight = jnp.maximum(0.0, 1.0 - jnp.abs(row_pos + 0.5 - centre) / span)
    inside = jnp.logical_and(row_pos >= first, row_pos < first + span_len)
    return jnp.where(inside, weight, 0.0)


def near_sum(blocks, cover_blocks):
    totals = blocks[:, 2]
    cover = cover_blocks[:, 2]
    for offset in (-2, -1, 1, 2):
        moved, moved_cover = from_behind(
            (blocks[:, offset + 2], cover_blocks[:, offset + 2]), "slab", offset
        )
        totals = totals + moved
        cover = cover + moved_cover
    return (totals, cover)


def halo_rows(own_rows):
    rows_dev = own_rows.shape[1]
    inner = own_rows
    result = own_rows
    for turn in range(2):
        if turn == 0:
            source = own_rows
        else:
            source = jnp.concatenate([inner[:, 2 * rows_dev :], inner[:, :rows_dev]], axis=1)
        grown = with_halo(source, (("slab", 1),), rows_dev)
        if turn == 0:
            inner = grown
        else:
            result = jnp.concatenate([grown[:, :rows_dev], inner, grown[:, -rows_dev:]], axis=1)
    return result


def body(volume, measured, foot_start, foot_len, order, ray_table):
    high = lax.Precision.HIGHEST
    slab_pos = lax.axis_index("slab")
    ang_pos = lax.axis_index("ang")
    per_dev = measured.shape[0]
    rows_dev = measured.shape[1]
    share = volume.shape[1]
    picked = order[:ANGLES]
    onehot = (picked[:, None] == jnp.arange(ray_table.shape[0], dtype=jnp.int32)[None, :]).astype(
        jnp.float32
    )
    weights_all = jnp.dot(onehot, ray_table, precision=high)
    weights_mine = lax.dynamic_slice_in_dim(weights_all, ang_pos * per_dev, per_dev, 0)
    path = weights_mine.sum(1)
    weights_cells = lax.dynamic_slice_in_dim(weights_all, ang_pos * share, share, 1)
    ray_part = jnp.einsum("ay,zyx->azx", weights_cells, volume, precision=high)
    summed = summed_on_arrival(ray_part, "ang", 0)
    starts = foot_start[0].astype(jnp.float32)
    lengths = foot_len[0].astype(jnp.float32)
    first_row = (slab_pos - 2) * rows_dev
    rows = (first_row + lax.iota(jnp.int32, 5 * rows_dev)).astype(jnp.float32)
    kernel = hat_weights(starts, lengths, rows)
    partial_value = jnp.einsum("arz,azx->arx", kernel, summed, precision=high)
    coverage = kernel.sum(-1)
    blocks = partial_value.reshape(per_dev, 5, rows_dev, partial_value.shape[2])
    cover_blocks = coverage.reshape(per_dev, 5, rows_dev)
    totals, cover = near_sum(blocks, cover_blocks)
    denom = jnp.maximum(path[:, None] * cover, 0.25)
    res_mine = (measured.astype(jnp.float32) - totals) / denom[:, :, None]
    res_rows = halo_rows(res_mine)
    back = jnp.einsum("arz,arx->azx", kernel, res_rows, precision=high)
    slice_weight = kernel.sum(1)
    back_all, slice_all = side_by_side((back, slice_weight), "ang", 0, 2)
    update = jnp.einsum("ay,azx->zyx", weights_cells, back_all, precision=high)
    column = jnp.einsum("ay,az->zy", weights_cells, slice_all, precision=high)
    updated = volume + update / column[:, :, None]
    return (updated, res_mine)


def solution(mesh):
    return jax.shard_map(
        body,
        mesh=mesh,
        in_specs=(
            P("slab", "ang", None),
            P("ang", "slab", None),
            P("slab", "ang"),
            P("slab", "ang"),
            P(),
            P(),
        ),
        out_specs=(P("slab", "ang", None), P("ang", "slab", None)),
        check_vma=False,
    )
```

profile of v0, /device:TPU:129, one launch (start us, length us, event | category | flops | bytes accessed | tf_op | source)
XLA Modules:
  0.0 156.6 jit_solution(16223021323724058961)
XLA Ops:
  2.3 3.9 %convolution_bitcast_fusion.1 = f32[8,1,8,4096]{3,0,2,1:T(8,128)S(1)} fusion(f32[8,32,4096]{2,1,0:T(8,128)} %param.6, f32[8,256]{1,0:T(8,128)S(1)} %fusion.30, s32[]{:T(128)S(6)} %select_n.45), kind=kOutput, calls=%fused_computation.4 | convolution fusion | flops 100663296 | bytes 5246980 | tf_op jit(solution)/shard_map/ay,zyx->azx/dot_general | solution.py:126
  7.8 5.1 %all-to-all-start = ((f32[8,1,8,4096]{3,2,1,0:T(8,128)}), f32[8,1,8,4096]{3,2,1,0:T(8,128)S(1)}, u32[]{:S(2)}, u32[]{:S(2)}) async-start(f32[8,1,8,4096]{3,2,1,0:T(8,128)} %copy.16), calls=%async_computation | async-start | bytes 2097152 | tf_op jit(solution)/shard_map/all_to_all | solution.py:38
  14.2 13.6 %all-to-all-done = f32[8,1,8,4096]{3,2,1,0:T(8,128)S(1)} async-done(((f32[8,1,8,4096]{3,2,1,0:T(8,128)}), f32[8,1,8,4096]{3,2,1,0:T(8,128)S(1)}, u32[]{:S(2)}, u32[]{:S(2)}) %all-to-all-start) | async-done | bytes 1048608 | tf_op jit(solution)/shard_map/all_to_all | solution.py:38
  27.9 2.3 %convolution_bitcast_fusion = f32[1,5,32,4096]{3,2,1,0:T(8,128)S(1)} fusion(f32[8,4096]{1,0:T(8,128)S(1)} %reduce_sum.36, f32[]{:T(128)} %bitcast.2, f32[8]{0:T(128)S(1)} %multiply_add_fusion, f32[5,32]{1,0:T(8,128)S(1)} %convert_add_fusion, pred[5,32]{1,0:T(8,128)(4,1)S(1)} %fusion.29), kind=kOutput, calls=%fused_computation | convolution fusion | flops 62922240 | bytes 2753348 | tf_op jit(solution)/shard_map/arz,azx->arx/dot_general | solution.py:133
  31.6 3.9 %collective-permute-start = (f32[1,32,4096]{2,1,0:T(8,128)}, f32[1,32,4096]{2,1,0:T(8,128)S(1)}, u32[]{:S(2)}, u32[]{:S(2)}) collective-permute-start(f32[1,32,4096]{2,1,0:T(8,128)} %get-tuple-element.4), channel_id=1, source_target_pairs={{16,0},{24,8},{32,16},{40,24},{48,32},{56,40},{64,48},{72,56},{80,... | collective-permute-start | bytes 1572872 | tf_op jit(solution)/shard_map/ppermute | solution.py:15
  35.5 3.0 %collective-permute-start.1 = (f32[1,32,4096]{2,1,0:T(8,128)}, f32[1,32,4096]{2,1,0:T(8,128)}, u32[]{:S(2)}, u32[]{:S(2)}) collective-permute-start(f32[1,32,4096]{2,1,0:T(8,128)} %get-tuple-element.7), channel_id=1, source_target_pairs={{8,0},{16,8},{24,16},{32,24},{40,32},{48,40},{56,48},{64,56},{72,6... | collective-permute-start | bytes 1572872 | tf_op jit(solution)/shard_map/ppermute | solution.py:15
  38.5 4.1 %collective-permute-start.2 = (f32[1,32,4096]{2,1,0:T(8,128)}, f32[1,32,4096]{2,1,0:T(8,128)}, u32[]{:S(2)}, u32[]{:S(2)}) collective-permute-start(f32[1,32,4096]{2,1,0:T(8,128)} %get-tuple-element.6), channel_id=1, source_target_pairs={{0,8},{8,16},{16,24},{24,32},{32,40},{40,48},{48,56},{56,64},{64,7... | collective-permute-start | bytes 1572872 | tf_op jit(solution)/shard_map/ppermute | solution.py:15
  42.6 4.0 %collective-permute-start.3 = (f32[1,32,4096]{2,1,0:T(8,128)}, f32[1,32,4096]{2,1,0:T(8,128)}, u32[]{:S(2)}, u32[]{:S(2)}) collective-permute-start(f32[1,32,4096]{2,1,0:T(8,128)} %get-tuple-element.5), channel_id=1, source_target_pairs={{0,16},{8,24},{16,32},{24,40},{32,48},{40,56},{48,64},{56,72},{64,... | collective-permute-start | bytes 1572872 | tf_op jit(solution)/shard_map/ppermute | solution.py:15
  46.8 4.9 %collective-permute-start.4 = (f32[1,32]{1,0:T(1,128)S(1)}, f32[1,32]{1,0:T(1,128)S(1)}, u32[]{:S(2)}, u32[]{:S(2)}) collective-permute-start(f32[1,32]{1,0:T(1,128)S(1)} %get-tuple-element.8), channel_id=1, source_target_pairs={{16,0},{24,8},{32,16},{40,24},{48,32},{56,40},{64,48},{72,56},{80,... | collective-permute-start | bytes 392 | tf_op jit(solution)/shard_map/ppermute | solution.py:15
  51.7 13.0 %collective-permute-done.4 = f32[1,32]{1,0:T(1,128)S(1)} collective-permute-done((f32[1,32]{1,0:T(1,128)S(1)}, f32[1,32]{1,0:T(1,128)S(1)}, u32[]{:S(2)}, u32[]{:S(2)}) %collective-permute-start.4) | collective-permute-done | bytes 160 | tf_op jit(solution)/shard_map/ppermute | solution.py:15
  64.7 9.2 %collective-permute-start.5 = (f32[1,32]{1,0:T(1,128)S(1)}, f32[1,32]{1,0:T(1,128)S(1)}, u32[]{:S(2)}, u32[]{:S(2)}) collective-permute-start(f32[1,32]{1,0:T(1,128)S(1)} %get-tuple-element.11), channel_id=1, source_target_pairs={{8,0},{16,8},{24,16},{32,24},{40,32},{48,40},{56,48},{64,56},{72,6... | collective-permute-start | bytes 392 | tf_op jit(solution)/shard_map/ppermute | solution.py:15
  74.7 1.9 %collective-permute-start.6 = (f32[1,32]{1,0:T(1,128)S(1)}, f32[1,32]{1,0:T(1,128)S(1)}, u32[]{:S(2)}, u32[]{:S(2)}) collective-permute-start(f32[1,32]{1,0:T(1,128)S(1)} %get-tuple-element.10), channel_id=1, source_target_pairs={{0,8},{8,16},{16,24},{24,32},{32,40},{40,48},{48,56},{56,64},{64,7... | collective-permute-start | bytes 392 | tf_op jit(solution)/shard_map/ppermute | solution.py:15
  77.8 5.6 %collective-permute-start.7 = (f32[1,32]{1,0:T(1,128)S(1)}, f32[1,32]{1,0:T(1,128)S(1)}, u32[]{:S(2)}, u32[]{:S(2)}) collective-permute-start(f32[1,32]{1,0:T(1,128)S(1)} %get-tuple-element.9), channel_id=1, source_target_pairs={{0,16},{8,24},{16,32},{24,40},{32,48},{40,56},{48,64},{56,72},{64,... | collective-permute-start | bytes 392 | tf_op jit(solution)/shard_map/ppermute | solution.py:15
  84.0 2.0 %collective-permute-done.7 = f32[1,32]{1,0:T(1,128)S(1)} collective-permute-done((f32[1,32]{1,0:T(1,128)S(1)}, f32[1,32]{1,0:T(1,128)S(1)}, u32[]{:S(2)}, u32[]{:S(2)}) %collective-permute-start.7) | collective-permute-done | bytes 160 | tf_op jit(solution)/shard_map/ppermute | solution.py:15
  87.4 1.7 %fusion.9 = f32[1,32,4096]{2,1,0:T(8,128)S(1)} fusion(f32[1,32,4096]{2,1,0:T(8,128)} %collective-permute-done.3, f32[1,32,4096]{2,1,0:T(8,128)} %collective-permute-done.2, f32[1,32,4096]{2,1,0:T(8,128)} %collective-permute-done.1, f32[1,32,4096]{2,1,0:T(8,128)} %copy-done.2, f32[1,5,32,4096]{3,2,1,0:T(8,128)S(1)} %convolution_bitcast_fusion, ...), kind=kLoop, calls=%fused_computation.19 | loop fusion | flops 917504 | bytes 3408000 | tf_op jit(solution)/shard_map/div | solution.py:139
  89.1 6.2 %collective-permute-start.8 = (f32[1,32,4096]{2,1,0:T(8,128)S(1)}, f32[1,32,4096]{2,1,0:T(8,128)S(1)}, u32[]{:S(2)}, u32[]{:S(2)}) collective-permute-start(f32[1,32,4096]{2,1,0:T(8,128)S(1)} %fusion.9), channel_id=1, source_target_pairs={{0,8},{8,16},{16,24},{24,32},{32,40},{40,48},{48,56},{56,64},{64,7... | collective-permute-start | bytes 1572872 | tf_op jit(solution)/shard_map/ppermute | solution.py:25
  95.3 4.4 %collective-permute-start.10 = (f32[1,32,4096]{2,1,0:T(8,128)S(1)}, f32[1,32,4096]{2,1,0:T(8,128)S(1)}, u32[]{:S(2)}, u32[]{:S(2)}) collective-permute-start(f32[1,32,4096]{2,1,0:T(8,128)S(1)} %fusion.9), channel_id=1, source_target_pairs={{8,0},{16,8},{24,16},{32,24},{40,32},{48,40},{56,48},{64,56},{72,6... | collective-permute-start | bytes 1572872 | tf_op jit(solution)/shard_map/ppermute | solution.py:26
  99.7 1.7 %collective-permute-done.8 = f32[1,32,4096]{2,1,0:T(8,128)S(1)} collective-permute-done((f32[1,32,4096]{2,1,0:T(8,128)S(1)}, f32[1,32,4096]{2,1,0:T(8,128)S(1)}, u32[]{:S(2)}, u32[]{:S(2)}) %collective-permute-start.8) | collective-permute-done | bytes 524320 | tf_op jit(solution)/shard_map/ppermute | solution.py:25
  101.4 5.9 %collective-permute-start.9 = (f32[1,32,4096]{2,1,0:T(8,128)S(1)}, f32[1,32,4096]{2,1,0:T(8,128)S(1)}, u32[]{:S(2)}, u32[]{:S(2)}) collective-permute-start(f32[1,32,4096]{2,1,0:T(8,128)S(1)} %collective-permute-done.8), channel_id=1, source_target_pairs={{0,8},{8,16},{16,24},{24,32},{32,40},{40,48},{48,56},{56,64},{64,7... | collective-permute-start | bytes 1572872 | tf_op jit(solution)/shard_map/ppermute | solution.py:25
  107.7 5.1 %collective-permute-done.10 = f32[1,32,4096]{2,1,0:T(8,128)S(1)} collective-permute-done((f32[1,32,4096]{2,1,0:T(8,128)S(1)}, f32[1,32,4096]{2,1,0:T(8,128)S(1)}, u32[]{:S(2)}, u32[]{:S(2)}) %collective-permute-start.10) | collective-permute-done | bytes 524320 | tf_op jit(solution)/shard_map/ppermute | solution.py:26
  112.9 1.9 %collective-permute-start.11 = (f32[1,32,4096]{2,1,0:T(8,128)S(1)}, f32[1,32,4096]{2,1,0:T(8,128)S(1)}, u32[]{:S(2)}, u32[]{:S(2)}) collective-permute-start(f32[1,32,4096]{2,1,0:T(8,128)S(1)} %collective-permute-done.10), channel_id=1, source_target_pairs={{8,0},{16,8},{24,16},{32,24},{40,32},{48,40},{56,48},{64,56},{72,6... | collective-permute-start | bytes 1572872 | tf_op jit(solution)/shard_map/ppermute | solution.py:26
  115.0 14.1 %collective-permute-done.11 = f32[1,32,4096]{2,1,0:T(8,128)S(1)} collective-permute-done((f32[1,32,4096]{2,1,0:T(8,128)S(1)}, f32[1,32,4096]{2,1,0:T(8,128)S(1)}, u32[]{:S(2)}, u32[]{:S(2)}) %collective-permute-start.11) | collective-permute-done | bytes 524320 | tf_op jit(solution)/shard_map/ppermute | solution.py:26
  130.6 18.0 %all_to_all.10 = f32[8,1,8,4097]{3,2,1,0:T(8,128)S(1)} all-to-all(f32[8,1,8,4097]{3,2,1,0:T(8,128)S(1)} %broadcast_in_dim.22), channel_id=1, replica_groups=mesh['slab'=32,'ang'=8] {'ang'}, dimensions={0} | all-to-all | bytes 2097664 | tf_op jit(solution)/shard_map/all_to_all | solution.py:50
  149.2 7.4 %fusion.1 = f32[8,32,4096]{2,1,0:T(8,128)} fusion(f32[8,32,4096]{2,1,0:T(8,128)} %param.6, f32[8,32]{1,0:T(8,128)S(1)} %fusion.25, f32[8,8,4097]{2,0,1:T(8,128)S(1)} %bitcast.81, f32[8,256]{1,0:T(8,128)S(1)} %fusion.30, s32[]{:T(128)S(6)} %select_n.45), kind=kOutput, calls=%fused_computation.3 | convolution fusion | flops 102760448 | bytes 9445380 | tf_op jit(solution)/shard_map/ay,azx->zyx/dot_general | solution.py:144
  (43 shorter events, 11.5 us)
Async XLA Ops:
  0.6 0.8 copy-start
  7.8 20.1 %all-to-all-start = ((f32[8,1,8,4096]{3,2,1,0:T(8,128)}), f32[8,1,8,4096]{3,2,1,0:T(8,128)S(1)}, u32[]{:S(2)}, u32[]{:S(2)}) async-start(f32[8,1,8,4096]{3,2,1,0:T(8,128)} %copy.16), calls=%async_computation | async-start | bytes 2097152 | tf_op jit(solution)/shard_map/all_to_all | solution.py:38
  30.2 57.2 %copy-start.3 = (bf16[1,32,4096]{2,1,0:T(8,128)(2,1)S(1)}, bf16[1,32,4096]{2,1,0:T(8,128)(2,1)}, u32[]{:S(2)}) copy-start(bf16[1,32,4096]{2,1,0:T(8,128)(2,1)} %param.7) | copy-start | bytes 786436
  31.6 55.0 %collective-permute-start = (f32[1,32,4096]{2,1,0:T(8,128)}, f32[1,32,4096]{2,1,0:T(8,128)S(1)}, u32[]{:S(2)}, u32[]{:S(2)}) collective-permute-start(f32[1,32,4096]{2,1,0:T(8,128)} %get-tuple-element.4), channel_id=1, source_target_pairs={{16,0},{24,8},{32,16},{40,24},{48,32},{56,40},{64,48},{72,56},{80,... | collective-permute-start | bytes 1572872 | tf_op jit(solution)/shard_map/ppermute | solution.py:15
  35.5 51.1 %collective-permute-start.1 = (f32[1,32,4096]{2,1,0:T(8,128)}, f32[1,32,4096]{2,1,0:T(8,128)}, u32[]{:S(2)}, u32[]{:S(2)}) collective-permute-start(f32[1,32,4096]{2,1,0:T(8,128)} %get-tuple-element.7), channel_id=1, source_target_pairs={{8,0},{16,8},{24,16},{32,24},{40,32},{48,40},{56,48},{64,56},{72,6... | collective-permute-start | bytes 1572872 | tf_op jit(solution)/shard_map/ppermute | solution.py:15
  38.5 48.2 %collective-permute-start.2 = (f32[1,32,4096]{2,1,0:T(8,128)}, f32[1,32,4096]{2,1,0:T(8,128)}, u32[]{:S(2)}, u32[]{:S(2)}) collective-permute-start(f32[1,32,4096]{2,1,0:T(8,128)} %get-tuple-element.6), channel_id=1, source_target_pairs={{0,8},{8,16},{16,24},{24,32},{32,40},{40,48},{48,56},{56,64},{64,7... | collective-permute-start | bytes 1572872 | tf_op jit(solution)/shard_map/ppermute | solution.py:15
  42.6 44.8 %collective-permute-start.3 = (f32[1,32,4096]{2,1,0:T(8,128)}, f32[1,32,4096]{2,1,0:T(8,128)}, u32[]{:S(2)}, u32[]{:S(2)}) collective-permute-start(f32[1,32,4096]{2,1,0:T(8,128)} %get-tuple-element.5), channel_id=1, source_target_pairs={{0,16},{8,24},{16,32},{24,40},{32,48},{40,56},{48,64},{56,72},{64,... | collective-permute-start | bytes 1572872 | tf_op jit(solution)/shard_map/ppermute | solution.py:15
  46.8 17.9 %collective-permute-start.4 = (f32[1,32]{1,0:T(1,128)S(1)}, f32[1,32]{1,0:T(1,128)S(1)}, u32[]{:S(2)}, u32[]{:S(2)}) collective-permute-start(f32[1,32]{1,0:T(1,128)S(1)} %get-tuple-element.8), channel_id=1, source_target_pairs={{16,0},{24,8},{32,16},{40,24},{48,32},{56,40},{64,48},{72,56},{80,... | collective-permute-start | bytes 392 | tf_op jit(solution)/shard_map/ppermute | solution.py:15
  64.7 10.0 %collective-permute-start.5 = (f32[1,32]{1,0:T(1,128)S(1)}, f32[1,32]{1,0:T(1,128)S(1)}, u32[]{:S(2)}, u32[]{:S(2)}) collective-permute-start(f32[1,32]{1,0:T(1,128)S(1)} %get-tuple-element.11), channel_id=1, source_target_pairs={{8,0},{16,8},{24,16},{32,24},{40,32},{48,40},{56,48},{64,56},{72,6... | collective-permute-start | bytes 392 | tf_op jit(solution)/shard_map/ppermute | solution.py:15
  74.7 3.0 %collective-permute-start.6 = (f32[1,32]{1,0:T(1,128)S(1)}, f32[1,32]{1,0:T(1,128)S(1)}, u32[]{:S(2)}, u32[]{:S(2)}) collective-permute-start(f32[1,32]{1,0:T(1,128)S(1)} %get-tuple-element.10), channel_id=1, source_target_pairs={{0,8},{8,16},{16,24},{24,32},{32,40},{40,48},{48,56},{56,64},{64,7... | collective-permute-start | bytes 392 | tf_op jit(solution)/shard_map/ppermute | solution.py:15
  77.8 8.3 %collective-permute-start.7 = (f32[1,32]{1,0:T(1,128)S(1)}, f32[1,32]{1,0:T(1,128)S(1)}, u32[]{:S(2)}, u32[]{:S(2)}) collective-permute-start(f32[1,32]{1,0:T(1,128)S(1)} %get-tuple-element.9), channel_id=1, source_target_pairs={{0,16},{8,24},{16,32},{24,40},{32,48},{40,56},{48,64},{56,72},{64,... | collective-permute-start | bytes 392 | tf_op jit(solution)/shard_map/ppermute | solution.py:15
  86.6 0.8 copy-start.2
  89.1 40.0 %copy-start.1 = (f32[1,32,4096]{2,1,0:T(8,128)}, f32[1,32,4096]{2,1,0:T(8,128)S(1)}, u32[]{:S(2)}) copy-start(f32[1,32,4096]{2,1,0:T(8,128)S(1)} %fusion.9) | copy-start | bytes 1572868
  89.1 12.3 %collective-permute-start.8 = (f32[1,32,4096]{2,1,0:T(8,128)S(1)}, f32[1,32,4096]{2,1,0:T(8,128)S(1)}, u32[]{:S(2)}, u32[]{:S(2)}) collective-permute-start(f32[1,32,4096]{2,1,0:T(8,128)S(1)} %fusion.9), channel_id=1, source_target_pairs={{0,8},{8,16},{16,24},{24,32},{32,40},{40,48},{48,56},{56,64},{64,7... | collective-permute-start | bytes 1572872 | tf_op jit(solution)/shard_map/ppermute | solution.py:25
  95.3 17.6 %collective-permute-start.10 = (f32[1,32,4096]{2,1,0:T(8,128)S(1)}, f32[1,32,4096]{2,1,0:T(8,128)S(1)}, u32[]{:S(2)}, u32[]{:S(2)}) collective-permute-start(f32[1,32,4096]{2,1,0:T(8,128)S(1)} %fusion.9), channel_id=1, source_target_pairs={{8,0},{16,8},{24,16},{32,24},{40,32},{48,40},{56,48},{64,56},{72,6... | collective-permute-start | bytes 1572872 | tf_op jit(solution)/shard_map/ppermute | solution.py:26
  101.4 13.4 %collective-permute-start.9 = (f32[1,32,4096]{2,1,0:T(8,128)S(1)}, f32[1,32,4096]{2,1,0:T(8,128)S(1)}, u32[]{:S(2)}, u32[]{:S(2)}) collective-permute-start(f32[1,32,4096]{2,1,0:T(8,128)S(1)} %collective-permute-done.8), channel_id=1, source_target_pairs={{0,8},{8,16},{16,24},{24,32},{32,40},{40,48},{48,56},{56,64},{64,7... | collective-permute-start | bytes 1572872 | tf_op jit(solution)/shard_map/ppermute | solution.py:25
  112.9 16.2 %collective-permute-start.11 = (f32[1,32,4096]{2,1,0:T(8,128)S(1)}, f32[1,32,4096]{2,1,0:T(8,128)S(1)}, u32[]{:S(2)}, u32[]{:S(2)}) collective-permute-start(f32[1,32,4096]{2,1,0:T(8,128)S(1)} %collective-permute-done.10), channel_id=1, source_target_pairs={{8,0},{16,8},{24,16},{32,24},{40,32},{48,40},{56,48},{64,56},{72,6... | collective-permute-start | bytes 1572872 | tf_op jit(solution)/shard_map/ppermute | solution.py:26
where the time goes:
time: 157 us
  starting transfers between devices  60 us (38%)
  waiting for transfers between devices  51.4 us (33%)
  blocking collectives  18 us (11%)
  matrix products  16 us (10%)
  local copies, waits for them, and re-layouts  5.29 us (3%)
  other arithmetic  3.58 us (2%)
  between operations  2.24 us (1%)
    ppermute x8, starting transfers between devices, from_behind(): lax.ppermute(value, axis, [(source, source + steps) for source in range(l...  36.5 us
    ppermute x2, waiting for transfers between devices, with_halo(): after = lax.ppermute(leading, axis, down)  19.2 us
    all_to_all x1, blocking collectives, copy_for_each(): lax.all_to_all(jnp.broadcast_to(value[None], (devices, *value.shape)), ax...  18 us
    ppermute x8, waiting for transfers between devices, from_behind(): lax.ppermute(value, axis, [(source, source + steps) for source in range(l...  16.9 us
    all_to_all x1, waiting for transfers between devices, summed_on_arrival(): lax.all_to_all(tiles, axis, split_axis=0, concat_axis=0, tiled=True)  13.6 us
    ppermute x2, starting transfers between devices, with_halo(): before = lax.ppermute(last, axis, up)  12 us
    dot_general x1, matrix products, body(): update = jnp.einsum('ay,azx->zyx', weights_cells, back_all, precision=high)  7.41 us
    ppermute x2, starting transfers between devices, with_halo(): after = lax.ppermute(leading, axis, down)  6.32 us
  transfers between devices with their start and end apart: 13, of which 8 were waited for; matrix products, arithmetic and copies ran while one was open for 1% of the time, Pallas kernels for 0%

commit v1 on v0

v1 whole, which is shorter than its diff:
```python
import functools

import jax
import jax.numpy as jnp
from jax import lax
from jax.experimental import pallas as pl
from jax.experimental.pallas import tpu as pltpu
from jax.sharding import PartitionSpec as P

ZDEV = 8
ANGLES = 8
CHUNKS = 8
UPDATE_COLUMNS = 512
MESH = pl.DeviceIdType.MESH
F32 = jnp.float32
BF16 = jnp.bfloat16

SIB, ODD, UP2, DOWN2 = range(4)
BACK = (SIB, ODD, DOWN2, UP2)
RAY, PAIR, SLAB, BACKPROJ, PAIR2, GATHER, MESSAGES = 0, 3, 4, 8, 12, 13, 16


def order_of_steps(chunks):
    wire = {0: ("y", 11.2), 1: ("x", 5.6), 2: ("s", 8.4), 3: ("s", 8.4), 4: ("x", 5.6), 5: ("y", 11.2)}
    work = {0: (2.4, 0.0), 1: (0.5, 0.1), 2: (0.3, 0.1), 3: (1.6, 0.4), 4: (0.3, 0.1), 5: (0.3, 0.1), 6: (0.0, 0.1)}
    free = {"y": 0.0, "x": 0.0, "s": 0.0}
    ready = {(0, c): 1.5 + 1.2 * (c + 1) / chunks for c in range(chunks)}
    now, steps = 0.0, []
    while ready:
        waiting = [k for k in ready if ready[k] <= now]
        if waiting:
            step = max(waiting, key=lambda k: (k[0], -k[1]))
        else:
            step = min(ready, key=lambda k: (ready[k], -k[0]))
        now = max(now, ready.pop(step)) + work[step[0]][0] / chunks + work[step[0]][1]
        steps.append(step)
        if step[0] in wire:
            link, total = wire[step[0]]
            begin = max(free[link], now)
            free[link] = begin + total / chunks
            ready[(step[0] + 1, step[1])] = free[link] + 2.2
    return steps


def hat(row, first, length, k):
    span = length / ZDEV
    centre = first + (k + 0.5) * span
    weight = jnp.maximum(0.0, 1.0 - jnp.abs(row + 0.5 - centre) / span)
    return jnp.where((row >= first) & (row < first + length), weight, 0.0)


def high_part(value):
    return value.astype(BF16).astype(F32)


def iota(shape, dim):
    return lax.broadcasted_iota(jnp.int32, shape, dim)


def exchange_kernel(
    chunks, width,
    order_ref, start_ref, length_ref, table_ref, volume_hbm, measured_hbm,
    residual_hbm, gathered_hbm, back_weights_hbm,
    vol, meas, part, ray_in, pair_out, pair_in, sums, sums_in, out_rows, back_out, back_in,
    both_out, both_in, gathered, params, neighbour_params, weights, picked,
    project_weights, spread_weights, scale, back_weights,
    load_sem, store_sem, send_sem, recv_sem, psend_sem, precv_sem,
):
    slab = lax.axis_index("slab")
    ang = lax.axis_index("ang")
    n_slab = lax.axis_size("slab")
    y = lax.rem(ang, 4)
    xl = ang // 4
    core = lax.rem(slab, 2)
    other = 1 - xl
    pair_dev = (slab, other * 4 + y)
    sib_dev = (slab + 1 - 2 * core, ang)
    odd_dev = (lax.rem(slab + 2 * core - 1 + n_slab, n_slab), other * 4 + y)
    up_dev = (lax.rem(slab + 2, n_slab), other * 4 + y)
    down_dev = (lax.rem(slab + n_slab - 2, n_slab), other * 4 + y)
    slab_devs = (sib_dev, odd_dev, up_dev, down_dev)
    y_of = [None] + [lax.rem(y + d, 4) for d in (1, 2, 3)]
    y_devs = [None] + [(slab, xl * 4 + y_of[d]) for d in (1, 2, 3)]

    loads = [
        pltpu.make_async_copy(volume_hbm.at[:, pl.ds(c * width, width)], vol.at[c], load_sem.at[c])
        for c in range(chunks)
    ]
    for copy in loads:
        copy.start()
    load_measured = pltpu.make_async_copy(measured_hbm, meas, load_sem.at[chunks])
    load_measured.start()

    barrier = pltpu.get_barrier_semaphore()
    greeted = (*y_devs[1:], pair_dev, *slab_devs)
    for device in greeted:
        pl.semaphore_signal(barrier, inc=1, device_id=device, device_id_type=MESH)

    first_here = jnp.full((8, 128), start_ref[0, 0], jnp.int32).astype(F32)
    length_here = jnp.full((8, 128), length_ref[0, 0], jnp.int32).astype(F32)
    params[y, xl, 0] = first_here
    params[y, xl, 1] = length_here

    for m in range(ANGLES):
        angle = (m % 2) * 4 + m // 2
        picked[pl.ds(m, 1), :] = table_ref[pl.ds(order_ref[angle], 1), :]
    cells = picked.shape[1]
    share = cells // 8
    pick = (iota((cells, cells), 0) == ang * share + lax.rem(iota((cells, cells), 1), share)).astype(F32)
    mine = jnp.dot(picked[...], pick, precision=lax.Precision.HIGHEST, preferred_element_type=F32)
    blocks = jnp.broadcast_to(mine[:, None, :], (ANGLES, ZDEV, cells)).reshape(ANGLES * ZDEV, cells)
    own_slice = lax.rem(iota(blocks.shape, 0), ZDEV) == iota(blocks.shape, 1) // share
    blocks = jnp.where(own_slice, blocks, 0.0)
    weights[...] = blocks
    blocks_high = high_part(blocks)
    ray_weights = jnp.concatenate([blocks_high, blocks - blocks_high], axis=0).astype(BF16)

    pl.semaphore_wait(barrier, len(greeted))

    def remote(src, dst, sem, c, device, out_sem=None):
        return pltpu.make_async_remote_copy(
            src_ref=src, dst_ref=dst,
            send_sem=send_sem.at[c, sem if out_sem is None else out_sem],
            recv_sem=recv_sem.at[c, sem], device_id=device, device_id_type=MESH,
        )

    def param_copy(src, dst, k, device):
        return pltpu.make_async_remote_copy(
            src_ref=src, dst_ref=dst, send_sem=psend_sem.at[k], recv_sem=precv_sem.at[k],
            device_id=device, device_id_type=MESH,
        )

    own_params = params.at[y, xl]
    param_first = [
        param_copy(own_params, own_params, 0, pair_dev),
        param_copy(own_params, neighbour_params.at[SIB], 1, sib_dev),
    ]
    param_second = [
        param_copy(params.at[y, other], neighbour_params.at[ODD], 2, odd_dev),
        param_copy(params.at[y, other], neighbour_params.at[DOWN2], 3, up_dev),
        param_copy(params.at[y, other], neighbour_params.at[UP2], 4, down_dev),
    ] + [param_copy(params.at[y], params.at[y], 4 + d, y_devs[d]) for d in (1, 2, 3)]
    for copy in param_first:
        copy.start()

    ray = [[remote(part.at[c, y_of[d]], ray_in.at[c, d - 1], RAY + d - 1, c, y_devs[d]) for d in (1, 2, 3)] for c in range(chunks)]
    pair = [remote(pair_out.at[c], pair_in.at[c], PAIR, c, pair_dev) for c in range(chunks)]
    to_slab = [
        [
            remote(sums.at[c, xl if k == SIB else other], sums_in.at[c, BACK[k]], SLAB + BACK[k], c, slab_devs[k], SLAB + k)
            for k in range(4)
        ]
        for c in range(chunks)
    ]
    to_back = [
        [
            remote(back_out.at[c, 1 + k], back_in.at[c, BACK[k]], BACKPROJ + BACK[k], c, slab_devs[k], BACKPROJ + k)
            for k in range(4)
        ]
        for c in range(chunks)
    ]
    pair2 = [remote(both_out.at[c], both_in.at[c], PAIR2, c, pair_dev) for c in range(chunks)]
    gather = [[remote(gathered.at[c, y], gathered.at[c, y], GATHER + d - 1, c, y_devs[d]) for d in (1, 2, 3)] for c in range(chunks)]
    stores = []

    def wait_in(copies):
        for copy in copies:
            copy.wait_recv()

    def tables():
        wait_in(param_second)
        tiles = [params[y, xl]] + [neighbour_params[k] for k in range(4)]
        rows = first_here.shape[0] * 4
        lane = iota((rows, 128), 1)
        row = (slab * rows + iota((rows, 128), 0)).astype(F32)
        third = (lane >= 40).astype(jnp.int32) + (lane >= 80).astype(jnp.int32) + (lane >= 120).astype(jnp.int32)
        within = lane - 40 * third
        role = lax.shift_right_logical(within, 3)
        first = jnp.zeros((rows, 128), F32)
        length = jnp.full((rows, 128), 32.0, F32)
        for k in range(5):
            first = jnp.where(role == k, tiles[k][0, 0:1, :], first)
            length = jnp.where(role == k, tiles[k][1, 0:1, :], length)
        weight = hat(row, first, length, lax.bitwise_and(within, 7).astype(F32))
        high = high_part(weight)
        project_weights[...] = jnp.where(third < 2, high, jnp.where(third == 2, weight - high, 0.0)).astype(BF16)
        coverage = jnp.sum(jnp.where(third == 0, weight, 0.0), axis=1, keepdims=True)
        path = jnp.sum(table_ref[pl.ds(order_ref[ang], 1), :], axis=1, keepdims=True)
        scale[...] = jnp.broadcast_to(1.0 / jnp.maximum(path * coverage, 0.25), scale.shape)
        lane = iota((8, 128), 1)
        quarter = lax.shift_right_logical(lane, 5)
        row = (slab * rows + lax.bitwise_and(lane, 31)).astype(F32)
        k8 = iota((8, 128), 0).astype(F32)
        spread = []
        for k in range(5):
            weight = hat(row, tiles[k][0], tiles[k][1], k8)
            high = high_part(weight)
            spread.append(jnp.where(quarter < 2, high, jnp.where(quarter == 2, weight - high, 0.0)))
        spread.append(jnp.zeros((8, 128), F32))
        spread_weights[...] = jnp.concatenate(spread, axis=0).astype(BF16)

    def update_weights():
        lane = iota((8, 128), 1)
        base = (slab - 2) * 32
        k8 = iota((8, 128), 0).astype(F32)
        column = jnp.zeros((8, cells), F32)
        for m in range(ANGLES):
            tile_first, tile_length = params[m // 2, m % 2, 0], params[m // 2, m % 2, 1]
            near = hat((base + lane).astype(F32), tile_first, tile_length, k8)
            far = hat((base + 128 + lane).astype(F32), tile_first, tile_length, k8)
            slice_weight = jnp.sum(near + far, axis=1, keepdims=True)
            column = column + weights[m * 8 : m * 8 + 8, :] * slice_weight
        column = jnp.sum(column, axis=0, keepdims=True)
        ratio = weights[...] / column
        high = high_part(ratio)
        stack = jnp.concatenate([high, high, ratio - high, jnp.zeros_like(high)], axis=0)
        back_weights[...] = stack.T.astype(BF16)
        copy = pltpu.make_async_copy(back_weights, back_weights_hbm, store_sem.at[2 * chunks])
        copy.start()
        stores.append(copy)

    def ray_sums(c):
        loads[c].wait()
        value = vol[c]
        high = value.astype(BF16)
        low = (value - high.astype(F32)).astype(BF16)
        first = jnp.dot(ray_weights, high, preferred_element_type=F32)
        second = jnp.dot(ray_weights[: ANGLES * ZDEV], low, preferred_element_type=F32)
        total = first[: ANGLES * ZDEV] + first[ANGLES * ZDEV :] + second
        part[c] = total.reshape(part.shape[1:])
        for copy in ray[c]:
            copy.start()

    def ray_arrived(c):
        wait_in(ray[c])
        pair_out[c] = part[c, y] + ray_in[c, 0] + ray_in[c, 1] + ray_in[c, 2]
        pair[c].start()

    def pair_arrived(c):
        wait_in([pair[c]])
        sums[c] = pair_out[c] + pair_in[c]
        for copy in to_slab[c]:
            copy.start()

    def project(c):
        wait_in(to_slab[c])
        five = jnp.concatenate([sums[c, xl]] + [sums_in[c, k] for k in range(4)], axis=0)
        high = high_part(five)
        stack = jnp.concatenate([high, five - high, high, jnp.zeros((8, width), F32)], axis=0).astype(BF16)
        projected = jnp.dot(project_weights[...], stack, preferred_element_type=F32)
        here = (meas[:, c * width : (c + 1) * width].astype(F32) - projected) * scale[:, 0:1]
        out_rows[c] = here
        high = high_part(here)
        stack = jnp.concatenate([high, here - high, high, jnp.zeros_like(high)], axis=0).astype(BF16)
        spread = jnp.dot(spread_weights[...], stack, preferred_element_type=F32)
        back_out[c] = spread[:40].reshape(back_out.shape[1:])
        for copy in to_back[c]:
            copy.start()
        copy = pltpu.make_async_copy(out_rows.at[c], residual_hbm.at[:, pl.ds(c * width, width)], store_sem.at[c])
        copy.start()
        stores.append(copy)

    def back_arrived(c):
        wait_in(to_back[c])
        both_out[c, xl] = back_out[c, 0] + back_in[c, SIB]
        both_out[c, other] = back_in[c, ODD] + back_in[c, UP2] + back_in[c, DOWN2]
        pair2[c].start()

    def pair2_arrived(c):
        wait_in([pair2[c]])
        gathered[c, y] = both_out[c] + both_in[c]
        for copy in gather[c]:
            copy.start()

    def gather_arrived(c):
        wait_in(gather[c])
        copy = pltpu.make_async_copy(gathered.at[c], gathered_hbm.at[:, :, :, pl.ds(c * width, width)], store_sem.at[chunks + c])
        copy.start()
        stores.append(copy)

    stages = (ray_sums, ray_arrived, pair_arrived, project, back_arrived, pair2_arrived, gather_arrived)
    forwarded = False
    done_tables = False
    done_update = False
    for stage, c in order_of_steps(chunks):
        if stage == 1 and not forwarded:
            wait_in(param_first)
            for copy in param_second:
                copy.start()
            forwarded = True
        if stage == 3 and not done_tables:
            load_measured.wait()
            tables()
            done_tables = True
        if stage == 4 and not done_update:
            update_weights()
            done_update = True
        stages[stage](c)

    for copy in param_first + param_second:
        copy.wait_send()
    for group in ray + to_slab + to_back + gather:
        for copy in group:
            copy.wait_send()
    for copy in pair + pair2:
        copy.wait_send()
    for copy in stores:
        copy.wait()


def update_kernel(weights_ref, volume_ref, gathered_ref, out_ref):
    value = gathered_ref[...]
    high = high_part(value)
    stack = jnp.concatenate([high, value - high, high, jnp.zeros_like(high)], axis=0).astype(BF16)
    out_ref[...] = volume_ref[...] + jnp.dot(weights_ref[...], stack, preferred_element_type=F32)


def body(volume, measured, foot_start, foot_len, order, ray_table):
    slices, share, columns = volume.shape
    cells = slices * share
    rows = measured.shape[1]
    flat = volume.reshape(cells, columns)
    chunks = CHUNKS
    width = columns // chunks
    vmem = pltpu.VMEM
    smem = pl.BlockSpec(memory_space=pltpu.SMEM)
    hbm = pl.BlockSpec(memory_space=pl.ANY)
    residual, gathered, back_weights = pl.pallas_call(
        functools.partial(exchange_kernel, chunks, width),
        out_shape=(
            jax.ShapeDtypeStruct((rows, columns), F32),
            jax.ShapeDtypeStruct((4, 2, ZDEV, columns), F32),
            jax.ShapeDtypeStruct((cells, 4 * ANGLES * ZDEV), BF16),
        ),
        in_specs=[smem, smem, smem, pl.BlockSpec(memory_space=pltpu.VMEM), hbm, hbm],
        out_specs=(hbm, hbm, hbm),
        scratch_shapes=[
            vmem((chunks, cells, width), F32),
            vmem((rows, columns), BF16),
            vmem((chunks, 4, 2, ZDEV, width), F32),
            vmem((chunks, 3, 2, ZDEV, width), F32),
            vmem((chunks, 2, ZDEV, width), F32),
            vmem((chunks, 2, ZDEV, width), F32),
            vmem((chunks, 2, ZDEV, width), F32),
            vmem((chunks, 4, ZDEV, width), F32),
            vmem((chunks, rows, width), F32),
            vmem((chunks, 5, ZDEV, width), F32),
            vmem((chunks, 4, ZDEV, width), F32),
            vmem((chunks, 2, ZDEV, width), F32),
            vmem((chunks, 2, ZDEV, width), F32),
            vmem((chunks, 4, 2, ZDEV, width), F32),
            vmem((4, 2, 2, 8, 128), F32),
            vmem((4, 2, 8, 128), F32),
            vmem((ANGLES * ZDEV, cells), F32),
            vmem((ANGLES, ray_table.shape[1]), F32),
            vmem((rows, 128), BF16),
            vmem((48, 128), BF16),
            vmem((rows, 128), F32),
            vmem((cells, 4 * ANGLES * ZDEV), BF16),
            pltpu.SemaphoreType.DMA((chunks + 1,)),
            pltpu.SemaphoreType.DMA((2 * chunks + 1,)),
            pltpu.SemaphoreType.DMA((chunks, MESSAGES)),
            pltpu.SemaphoreType.DMA((chunks, MESSAGES)),
            pltpu.SemaphoreType.DMA((8,)),
            pltpu.SemaphoreType.DMA((8,)),
        ],
        compiler_params=pltpu.CompilerParams(
            collective_id=0, has_side_effects=True, vmem_limit_bytes=40 * 1024 * 1024
        ),
        name="exchange",
    )(order, foot_start, foot_len, ray_table, flat, measured.reshape(rows, columns))
    block = UPDATE_COLUMNS
    updated = pl.pallas_call(
        update_kernel,
        out_shape=jax.ShapeDtypeStruct((cells, columns), F32),
        grid=(columns // block,),
        in_specs=[
            pl.BlockSpec((cells, 4 * ANGLES * ZDEV), lambda i: (0, 0)),
            pl.BlockSpec((cells, block), lambda i: (0, i)),
            pl.BlockSpec((ANGLES * ZDEV, block), lambda i: (0, i)),
        ],
        out_specs=pl.BlockSpec((cells, block), lambda i: (0, i)),
        name="update",
    )(back_weights, flat, gathered.reshape(ANGLES * ZDEV, columns))
    return (updated.reshape(slices, share, columns), residual.reshape(measured.shape))


def solution(mesh):
    return jax.shard_map(
        body,
        mesh=mesh,
        in_specs=(
            P("slab", "ang", None),
            P("ang", "slab", None),
            P("slab", "ang"),
            P("slab", "ang"),
            P(),
            P(),
        ),
        out_specs=(P("slab", "ang", None), P("ang", "slab", None)),
        check_vma=False,
    )
```

time: 157 us -> 68.9 us (0.44)
  the two profiles are of different devices: /device:TPU:129 before, /device:TPU:2 now
where the time goes in v1:
time: 68.9 us; the launch traced here: 68.5 us
  Pallas kernels  59.5 us (86%)
  local copies, waits for them, and re-layouts  7.04 us (10%)
  between operations  1.95 us (3%)
    pallas_call x1, Pallas kernels, body(): pl.pallas_call(functools.partial(exchange_kernel, chunks, width), out_sha...  52 us
    pallas_call x1, Pallas kernels, body(): pl.pallas_call(update_kernel, out_shape=jax.ShapeDtypeStruct((cells, colu...  7.47 us
    unnamed x13, local copies, waits for them, and re-layouts  7.04 us

profile of v1, /device:TPU:2, one launch (start us, length us, event | category | flops | bytes accessed | tf_op | source)
XLA Modules:
  0.0 68.5 jit_solution(10776639611213358113)
XLA Ops:
  1.9 0.0 copy-start
  1.9 2.2 %copy-done = f32[8,32,4096]{2,1,0:T(8,128)S(1)} copy-done((f32[8,32,4096]{2,1,0:T(8,128)S(1)}, f32[8,32,4096]{2,1,0:T(8,128)}, u32[]{:S(2)}) %copy-start) | copy-done | bytes 4194328
  4.1 0.0 copy-start.2
  4.1 0.9 %copy-done.2 = bf16[1,32,4096]{2,1,0:T(8,128)(2,1)S(1)} copy-done((bf16[1,32,4096]{2,1,0:T(8,128)(2,1)S(1)}, bf16[1,32,4096]{2,1,0:T(8,128)(2,1)}, u32[]{:S(2)}) %copy-start.2) | copy-done | bytes 262168
  5.1 0.0 copy-start.4
  5.1 0.8 %copy-done.4 = f32[64,256]{1,0:T(8,128)S(1)} copy-done((f32[64,256]{1,0:T(8,128)S(1)}, f32[64,256]{1,0:T(8,128)}, u32[]{:S(2)}) %copy-start.4) | copy-done | bytes 65560
  5.9 0.0 copy-start.5
  5.9 0.7 copy-done.5
  6.6 52.0 %exchange.1 = (f32[32,4096]{1,0:T(8,128)S(1)}, f32[4,2,8,4096]{3,2,1,0:T(8,128)S(1)}, bf16[256,256]{1,0:T(8,128)(2,1)S(1)}) custom-call(s32[64]{0:T(128)S(1)} %copy-done.5, s32[1,1]{1,0:T(1,128)S(6)} %copy.9.start_ref, s32[1,1]{1,0:T(1,128)S(6)} %copy.10.length_ref, f32[64,256]{1,0:T(8,128)S(1)} %copy-done.4, f32[256,4096]{1,0:T(8,128)S(1)} %bitcast.6, ...), custom_call_target="tpu_custom_call" | custom-call | tf_op jit(solution)/shard_map/exchange/pallas_call | solution.py:328
  58.6 0.0 copy-start.1
  58.6 1.0 %copy-done.1 = f32[4,2,8,4096]{3,2,1,0:T(8,128)} copy-done((f32[4,2,8,4096]{3,2,1,0:T(8,128)}, f32[4,2,8,4096]{3,2,1,0:T(8,128)S(1)}, u32[]{:S(2)}) %copy-start.1) | copy-done | bytes 1048600
  59.6 0.0 copy-start.3
  59.6 0.7 copy-done.3
  60.2 7.5 %update.1 = f32[256,4096]{1,0:T(8,128)} custom-call(bf16[256,256]{1,0:T(8,128)(2,1)} %copy-done.3, f32[256,4096]{1,0:T(8,128)} %bitcast.5, f32[64,4096]{1,0:T(8,128)} %bitcast.7), custom_call_target="tpu_custom_call" | custom-call | tf_op jit(solution)/shard_map/update/pallas_call | solution.py:373
  67.7 0.8 %copy.11 = f32[1,32,4096]{2,1,0:T(8,128)} copy(f32[1,32,4096]{2,1,0:T(8,128)S(1)} %bitcast.8) | data formatting | bytes 1048576
Async XLA Ops:
  1.9 2.2 %copy-start = (f32[8,32,4096]{2,1,0:T(8,128)S(1)}, f32[8,32,4096]{2,1,0:T(8,128)}, u32[]{:S(2)}) copy-start(f32[8,32,4096]{2,1,0:T(8,128)} %param.6) | copy-start | bytes 12582916
  4.1 0.9 %copy-start.2 = (bf16[1,32,4096]{2,1,0:T(8,128)(2,1)S(1)}, bf16[1,32,4096]{2,1,0:T(8,128)(2,1)}, u32[]{:S(2)}) copy-start(bf16[1,32,4096]{2,1,0:T(8,128)(2,1)} %param.7) | copy-start | bytes 786436
  5.1 0.8 %copy-start.4 = (f32[64,256]{1,0:T(8,128)S(1)}, f32[64,256]{1,0:T(8,128)}, u32[]{:S(2)}) copy-start(f32[64,256]{1,0:T(8,128)} %table_ref.1) | copy-start | bytes 196612
  5.9 0.7 copy-start.5
  58.6 1.0 %copy-start.1 = (f32[4,2,8,4096]{3,2,1,0:T(8,128)}, f32[4,2,8,4096]{3,2,1,0:T(8,128)S(1)}, u32[]{:S(2)}) copy-start(f32[4,2,8,4096]{3,2,1,0:T(8,128)S(1)} %get-tuple-element.6) | copy-start | bytes 3145732
  59.6 0.7 copy-start.3

commit v2 on v1

--- a/solution.py
+++ b/solution.py
@@ -10,7 +10,6 @@
 ZDEV = 8
 ANGLES = 8
 CHUNKS = 8
-UPDATE_COLUMNS = 512
 MESH = pl.DeviceIdType.MESH
 F32 = jnp.float32
 BF16 = jnp.bfloat16
@@ -59,12 +58,12 @@
 
 def exchange_kernel(
     chunks, width,
-    order_ref, start_ref, length_ref, table_ref, volume_hbm, measured_hbm,
-    residual_hbm, gathered_hbm, back_weights_hbm,
-    vol, meas, part, ray_in, pair_out, pair_in, sums, sums_in, out_rows, back_out, back_in,
+    start_ref, length_ref, order_hbm, table_hbm, volume_hbm, measured_hbm,
+    updated_ref, residual_ref,
+    vol, meas, order_ref, table_ref, part, ray_in, pair_out, pair_in, sums, sums_in, back_out, back_in,
     both_out, both_in, gathered, params, neighbour_params, weights, picked,
     project_weights, spread_weights, scale, back_weights,
-    load_sem, store_sem, send_sem, recv_sem, psend_sem, precv_sem,
+    load_sem, send_sem, recv_sem, psend_sem, precv_sem,
 ):
     slab = lax.axis_index("slab")
     ang = lax.axis_index("ang")
@@ -82,6 +81,10 @@
     y_of = [None] + [lax.rem(y + d, 4) for d in (1, 2, 3)]
     y_devs = [None] + [(slab, xl * 4 + y_of[d]) for d in (1, 2, 3)]
 
+    load_order = pltpu.make_async_copy(order_hbm, order_ref, load_sem.at[chunks + 2])
+    load_order.start()
+    load_table = pltpu.make_async_copy(table_hbm, table_ref, load_sem.at[chunks + 1])
+    load_table.start()
     loads = [
         pltpu.make_async_copy(volume_hbm.at[:, pl.ds(c * width, width)], vol.at[c], load_sem.at[c])
         for c in range(chunks)
@@ -101,6 +104,8 @@
     params[y, xl, 0] = first_here
     params[y, xl, 1] = length_here
 
+    load_order.wait()
+    load_table.wait()
     for m in range(ANGLES):
         angle = (m % 2) * 4 + m // 2
         picked[pl.ds(m, 1), :] = table_ref[pl.ds(order_ref[angle], 1), :]
@@ -161,8 +166,6 @@
     ]
     pair2 = [remote(both_out.at[c], both_in.at[c], PAIR2, c, pair_dev) for c in range(chunks)]
     gather = [[remote(gathered.at[c, y], gathered.at[c, y], GATHER + d - 1, c, y_devs[d]) for d in (1, 2, 3)] for c in range(chunks)]
-    stores = []
-
     def wait_in(copies):
         for copy in copies:
             copy.wait_recv()
@@ -215,9 +218,6 @@
         high = high_part(ratio)
         stack = jnp.concatenate([high, high, ratio - high, jnp.zeros_like(high)], axis=0)
         back_weights[...] = stack.T.astype(BF16)
-        copy = pltpu.make_async_copy(back_weights, back_weights_hbm, store_sem.at[2 * chunks])
-        copy.start()
-        stores.append(copy)
 
     def ray_sums(c):
         loads[c].wait()
@@ -249,16 +249,13 @@
         stack = jnp.concatenate([high, five - high, high, jnp.zeros((8, width), F32)], axis=0).astype(BF16)
         projected = jnp.dot(project_weights[...], stack, preferred_element_type=F32)
         here = (meas[:, c * width : (c + 1) * width].astype(F32) - projected) * scale[:, 0:1]
-        out_rows[c] = here
+        residual_ref[:, c * width : (c + 1) * width] = here
         high = high_part(here)
         stack = jnp.concatenate([high, here - high, high, jnp.zeros_like(high)], axis=0).astype(BF16)
         spread = jnp.dot(spread_weights[...], stack, preferred_element_type=F32)
         back_out[c] = spread[:40].reshape(back_out.shape[1:])
         for copy in to_back[c]:
             copy.start()
-        copy = pltpu.make_async_copy(out_rows.at[c], residual_hbm.at[:, pl.ds(c * width, width)], store_sem.at[c])
-        copy.start()
-        stores.append(copy)
 
     def back_arrived(c):
         wait_in(to_back[c])
@@ -274,9 +271,11 @@
 
     def gather_arrived(c):
         wait_in(gather[c])
-        copy = pltpu.make_async_copy(gathered.at[c], gathered_hbm.at[:, :, :, pl.ds(c * width, width)], store_sem.at[chunks + c])
-        copy.start()
-        stores.append(copy)
+        value = gathered[c].reshape(ANGLES * ZDEV, width)
+        high = high_part(value)
+        stack = jnp.concatenate([high, value - high, high, jnp.zeros_like(high)], axis=0).astype(BF16)
+        update = jnp.dot(back_weights[...], stack, preferred_element_type=F32)
+        updated_ref[:, c * width : (c + 1) * width] = vol[c] + update
 
     stages = (ray_sums, ray_arrived, pair_arrived, project, back_arrived, pair2_arrived, gather_arrived)
     forwarded = False
@@ -304,15 +303,6 @@
             copy.wait_send()
     for copy in pair + pair2:
         copy.wait_send()
-    for copy in stores:
-        copy.wait()
-
-
-def update_kernel(weights_ref, volume_ref, gathered_ref, out_ref):
-    value = gathered_ref[...]
-    high = high_part(value)
-    stack = jnp.concatenate([high, value - high, high, jnp.zeros_like(high)], axis=0).astype(BF16)
-    out_ref[...] = volume_ref[...] + jnp.dot(weights_ref[...], stack, preferred_element_type=F32)
 
 
 def body(volume, measured, foot_start, foot_len, order, ray_table):
@@ -324,26 +314,26 @@
     width = columns // chunks
     vmem = pltpu.VMEM
     smem = pl.BlockSpec(memory_space=pltpu.SMEM)
-    hbm = pl.BlockSpec(memory_space=pl.ANY)
-    residual, gathered, back_weights = pl.pallas_call(
+    hbm = pl.BlockSpec(memory_space=pltpu.HBM)
+    updated, residual = pl.pallas_call(
         functools.partial(exchange_kernel, chunks, width),
         out_shape=(
+            jax.ShapeDtypeStruct((cells, columns), F32),
             jax.ShapeDtypeStruct((rows, columns), F32),
-            jax.ShapeDtypeStruct((4, 2, ZDEV, columns), F32),
-            jax.ShapeDtypeStruct((cells, 4 * ANGLES * ZDEV), BF16),
         ),
-        in_specs=[smem, smem, smem, pl.BlockSpec(memory_space=pltpu.VMEM), hbm, hbm],
-        out_specs=(hbm, hbm, hbm),
+        in_specs=[smem, smem, hbm, hbm, hbm, hbm],
+        out_specs=(pl.BlockSpec(memory_space=pltpu.VMEM),) * 2,
         scratch_shapes=[
             vmem((chunks, cells, width), F32),
             vmem((rows, columns), BF16),
+            pltpu.SMEM(order.shape, jnp.int32),
+            vmem(ray_table.shape, F32),
             vmem((chunks, 4, 2, ZDEV, width), F32),
             vmem((chunks, 3, 2, ZDEV, width), F32),
             vmem((chunks, 2, ZDEV, width), F32),
             vmem((chunks, 2, ZDEV, width), F32),
             vmem((chunks, 2, ZDEV, width), F32),
             vmem((chunks, 4, ZDEV, width), F32),
-            vmem((chunks, rows, width), F32),
             vmem((chunks, 5, ZDEV, width), F32),
             vmem((chunks, 4, ZDEV, width), F32),
             vmem((chunks, 2, ZDEV, width), F32),
@@ -357,8 +347,7 @@
             vmem((48, 128), BF16),
             vmem((rows, 128), F32),
             vmem((cells, 4 * ANGLES * ZDEV), BF16),
-            pltpu.SemaphoreType.DMA((chunks + 1,)),
-            pltpu.SemaphoreType.DMA((2 * chunks + 1,)),
+            pltpu.SemaphoreType.DMA((chunks + 3,)),
             pltpu.SemaphoreType.DMA((chunks, MESSAGES)),
             pltpu.SemaphoreType.DMA((chunks, MESSAGES)),
             pltpu.SemaphoreType.DMA((8,)),
@@ -368,20 +357,12 @@
             collective_id=0, has_side_effects=True, vmem_limit_bytes=40 * 1024 * 1024
         ),
         name="exchange",
-    )(order, foot_start, foot_len, ray_table, flat, measured.reshape(rows, columns))
-    block = UPDATE_COLUMNS
-    updated = pl.pallas_call(
-        update_kernel,
-        out_shape=jax.ShapeDtypeStruct((cells, columns), F32),
-        grid=(columns // block,),
-        in_specs=[
-            pl.BlockSpec((cells, 4 * ANGLES * ZDEV), lambda i: (0, 0)),
-            pl.BlockSpec((cells, block), lambda i: (0, i)),
-            pl.BlockSpec((ANGLES * ZDEV, block), lambda i: (0, i)),
-        ],
-        out_specs=pl.BlockSpec((cells, block), lambda i: (0, i)),
-        name="update",
-    )(back_weights, flat, gathered.reshape(ANGLES * ZDEV, columns))
+    )(
+        foot_start, foot_len, *(
+            pltpu.with_memory_space_constraint(a, pltpu.HBM)
+            for a in (order, ray_table, flat, measured.reshape(rows, columns))
+        )
+    )
     return (updated.reshape(slices, share, columns), residual.reshape(measured.shape))
 
 

time: 68.9 us -> 56.3 us (0.82)
  Pallas kernels: 59.5 us -> 51.4 us
  local copies, waits for them, and re-layouts: 7.04 us -> 2.81 us
    pallas_call x1 -> x0, Pallas kernels: 7.47 us -> none  [body(): pl.pallas_call(update_kernel, out_shape=jax.ShapeDtypeStruct((cells, colu...]
    unnamed x13 -> x2, local copies, waits for them, and re-layouts: 7.04 us -> 2.81 us
where the time goes in v2:
time: 56.3 us; the launch traced here: 56.2 us
  Pallas kernels  51.4 us (91%)
  local copies, waits for them, and re-layouts  2.81 us (5%)
  between operations  1.93 us (3%)
    pallas_call x1, Pallas kernels, body(): pl.pallas_call(functools.partial(exchange_kernel, chunks, width), out_sha...  51.4 us
    unnamed x2, local copies, waits for them, and re-layouts  2.81 us

profile of v2, /device:TPU:2, one launch (start us, length us, event | category | flops | bytes accessed | tf_op | source)
XLA Modules:
  0.0 56.2 jit_solution(24333846110340092)
XLA Ops:
  1.9 51.4 %exchange.1 = (f32[256,4096]{1,0:T(8,128)S(1)}, f32[32,4096]{1,0:T(8,128)S(1)}) custom-call(s32[1,1]{1,0:T(1,128)S(6)} %copy.10.start_ref, s32[1,1]{1,0:T(1,128)S(6)} %copy.11.length_ref, s32[64]{0:T(128)} %order_hbm.1, f32[64,256]{1,0:T(8,128)} %table_hbm.1, f32[256,4096]{1,0:T(8,128)} %bitcast.6, bf16[32,4096]{1,0:T(8,128)(2,1)} %bitcast.7), custom_call_target="tpu_custom_call" | custom-call | tf_op jit(solution)/shard_map/exchange/pallas_call | solution.py:318
  53.3 2.0 %copy.12 = f32[8,32,4096]{2,1,0:T(8,128)} copy(f32[8,32,4096]{2,1,0:T(8,128)S(1)} %bitcast.4) | data formatting | bytes 8388608
  55.4 0.8 %copy.13 = f32[1,32,4096]{2,1,0:T(8,128)} copy(f32[1,32,4096]{2,1,0:T(8,128)S(1)} %bitcast.5) | data formatting | bytes 1048576

commit v3 on v2

--- a/solution.py
+++ b/solution.py
@@ -10,35 +10,21 @@
 ZDEV = 8
 ANGLES = 8
 CHUNKS = 8
+LAG = 2.5
 MESH = pl.DeviceIdType.MESH
 F32 = jnp.float32
 BF16 = jnp.bfloat16
 
 SIB, ODD, UP2, DOWN2 = range(4)
 BACK = (SIB, ODD, DOWN2, UP2)
-RAY, PAIR, SLAB, BACKPROJ, PAIR2, GATHER, MESSAGES = 0, 3, 4, 8, 12, 13, 16
+FAR_FIRST = (UP2, DOWN2, ODD, SIB)
+RAY, PAIR, SLAB, BACKPROJ, PAIR2, GATHER, EXCHANGES = range(7)
+SENT_ROWS = (48, 16, 32, 32, 16, 48)
 
 
 def order_of_steps(chunks):
-    wire = {0: ("y", 11.2), 1: ("x", 5.6), 2: ("s", 8.4), 3: ("s", 8.4), 4: ("x", 5.6), 5: ("y", 11.2)}
-    work = {0: (2.4, 0.0), 1: (0.5, 0.1), 2: (0.3, 0.1), 3: (1.6, 0.4), 4: (0.3, 0.1), 5: (0.3, 0.1), 6: (0.0, 0.1)}
-    free = {"y": 0.0, "x": 0.0, "s": 0.0}
-    ready = {(0, c): 1.5 + 1.2 * (c + 1) / chunks for c in range(chunks)}
-    now, steps = 0.0, []
-    while ready:
-        waiting = [k for k in ready if ready[k] <= now]
-        if waiting:
-            step = max(waiting, key=lambda k: (k[0], -k[1]))
-        else:
-            step = min(ready, key=lambda k: (ready[k], -k[0]))
-        now = max(now, ready.pop(step)) + work[step[0]][0] / chunks + work[step[0]][1]
-        steps.append(step)
-        if step[0] in wire:
-            link, total = wire[step[0]]
-            begin = max(free[link], now)
-            free[link] = begin + total / chunks
-            ready[(step[0] + 1, step[1])] = free[link] + 2.2
-    return steps
+    steps = [(k, c) for k in range(7) for c in range(chunks)]
+    return sorted(steps, key=lambda step: (step[1] + LAG * step[0], -step[0]))
 
 
 def hat(row, first, length, k):
@@ -122,11 +108,10 @@
 
     pl.semaphore_wait(barrier, len(greeted))
 
-    def remote(src, dst, sem, c, device, out_sem=None):
+    def remote(src, dst, exchange, c, device):
         return pltpu.make_async_remote_copy(
-            src_ref=src, dst_ref=dst,
-            send_sem=send_sem.at[c, sem if out_sem is None else out_sem],
-            recv_sem=recv_sem.at[c, sem], device_id=device, device_id_type=MESH,
+            src_ref=src, dst_ref=dst, send_sem=send_sem.at[exchange], recv_sem=recv_sem.at[c, exchange],
+            device_id=device, device_id_type=MESH,
         )
 
     def param_copy(src, dst, k, device):
@@ -148,27 +133,27 @@
     for copy in param_first:
         copy.start()
 
-    ray = [[remote(part.at[c, y_of[d]], ray_in.at[c, d - 1], RAY + d - 1, c, y_devs[d]) for d in (1, 2, 3)] for c in range(chunks)]
+    ray = [[remote(part.at[c, y_of[d]], ray_in.at[c, d - 1], RAY, c, y_devs[d]) for d in (1, 2, 3)] for c in range(chunks)]
     pair = [remote(pair_out.at[c], pair_in.at[c], PAIR, c, pair_dev) for c in range(chunks)]
     to_slab = [
-        [
-            remote(sums.at[c, xl if k == SIB else other], sums_in.at[c, BACK[k]], SLAB + BACK[k], c, slab_devs[k], SLAB + k)
-            for k in range(4)
-        ]
+        [remote(sums.at[c, xl if k == SIB else other], sums_in.at[c, BACK[k]], SLAB, c, slab_devs[k]) for k in FAR_FIRST]
         for c in range(chunks)
     ]
     to_back = [
-        [
-            remote(back_out.at[c, 1 + k], back_in.at[c, BACK[k]], BACKPROJ + BACK[k], c, slab_devs[k], BACKPROJ + k)
-            for k in range(4)
-        ]
+        [remote(back_out.at[c, 1 + k], back_in.at[c, BACK[k]], BACKPROJ, c, slab_devs[k]) for k in FAR_FIRST]
         for c in range(chunks)
     ]
     pair2 = [remote(both_out.at[c], both_in.at[c], PAIR2, c, pair_dev) for c in range(chunks)]
-    gather = [[remote(gathered.at[c, y], gathered.at[c, y], GATHER + d - 1, c, y_devs[d]) for d in (1, 2, 3)] for c in range(chunks)]
+    gather = [[remote(gathered.at[c, y], gathered.at[c, y], GATHER, c, y_devs[d]) for d in (1, 2, 3)] for c in range(chunks)]
+    landing = (ray_in, pair_in, sums_in, back_in, both_in, gathered.at[:, pl.ds(0, 3)])
+
     def wait_in(copies):
         for copy in copies:
             copy.wait_recv()
+
+    def wait_exchange(exchange, c):
+        whole = landing[exchange].at[c]
+        remote(whole, whole, exchange, c, pair_dev).wait_recv()
 
     def tables():
         wait_in(param_second)
@@ -232,18 +217,18 @@
             copy.start()
 
     def ray_arrived(c):
-        wait_in(ray[c])
+        wait_exchange(RAY, c)
         pair_out[c] = part[c, y] + ray_in[c, 0] + ray_in[c, 1] + ray_in[c, 2]
         pair[c].start()
 
     def pair_arrived(c):
-        wait_in([pair[c]])
+        wait_exchange(PAIR, c)
         sums[c] = pair_out[c] + pair_in[c]
         for copy in to_slab[c]:
             copy.start()
 
     def project(c):
-        wait_in(to_slab[c])
+        wait_exchange(SLAB, c)
         five = jnp.concatenate([sums[c, xl]] + [sums_in[c, k] for k in range(4)], axis=0)
         high = high_part(five)
         stack = jnp.concatenate([high, five - high, high, jnp.zeros((8, width), F32)], axis=0).astype(BF16)
@@ -258,19 +243,19 @@
             copy.start()
 
     def back_arrived(c):
-        wait_in(to_back[c])
+        wait_exchange(BACKPROJ, c)
         both_out[c, xl] = back_out[c, 0] + back_in[c, SIB]
         both_out[c, other] = back_in[c, ODD] + back_in[c, UP2] + back_in[c, DOWN2]
         pair2[c].start()
 
     def pair2_arrived(c):
-        wait_in([pair2[c]])
+        wait_exchange(PAIR2, c)
         gathered[c, y] = both_out[c] + both_in[c]
         for copy in gather[c]:
             copy.start()
 
     def gather_arrived(c):
-        wait_in(gather[c])
+        wait_exchange(GATHER, c)
         value = gathered[c].reshape(ANGLES * ZDEV, width)
         high = high_part(value)
         stack = jnp.concatenate([high, value - high, high, jnp.zeros_like(high)], axis=0).astype(BF16)
@@ -298,11 +283,9 @@
 
     for copy in param_first + param_second:
         copy.wait_send()
-    for group in ray + to_slab + to_back + gather:
-        for copy in group:
-            copy.wait_send()
-    for copy in pair + pair2:
-        copy.wait_send()
+    for exchange in range(EXCHANGES):
+        sent = vol.at[:, pl.ds(0, SENT_ROWS[exchange])]
+        remote(sent, sent, exchange, 0, pair_dev).wait_send()
 
 
 def body(volume, measured, foot_start, foot_len, order, ray_table):
@@ -348,8 +331,8 @@
             vmem((rows, 128), F32),
             vmem((cells, 4 * ANGLES * ZDEV), BF16),
             pltpu.SemaphoreType.DMA((chunks + 3,)),
-            pltpu.SemaphoreType.DMA((chunks, MESSAGES)),
-            pltpu.SemaphoreType.DMA((chunks, MESSAGES)),
+            pltpu.SemaphoreType.DMA((EXCHANGES,)),
+            pltpu.SemaphoreType.DMA((chunks, EXCHANGES)),
             pltpu.SemaphoreType.DMA((8,)),
             pltpu.SemaphoreType.DMA((8,)),
         ],

time: 56.3 us -> 53.4 us (0.948); the launches traced: 56.2 us -> 52.5 us
  Pallas kernels: 51.4 us -> 47.8 us
    pallas_call x1, Pallas kernels: 51.4 us -> 47.8 us  [body(): pl.pallas_call(functools.partial(exchange_kernel, chunks, width), out_sha...]
where the time goes in v3:
time: 53.4 us; the launch traced here: 52.5 us
  Pallas kernels  47.8 us (90%)
  local copies, waits for them, and re-layouts  2.81 us (5%)
  between operations  1.93 us (4%)
    pallas_call x1, Pallas kernels, body(): pl.pallas_call(functools.partial(exchange_kernel, chunks, width), out_sha...  47.8 us
    unnamed x2, local copies, waits for them, and re-layouts  2.81 us

profile of v3, /device:TPU:2, one launch (start us, length us, event | category | flops | bytes accessed | tf_op | source)
XLA Modules:
  0.0 52.5 jit_solution(14912542775715305293)
XLA Ops:
  1.9 47.8 %exchange.1 = (f32[256,4096]{1,0:T(8,128)S(1)}, f32[32,4096]{1,0:T(8,128)S(1)}) custom-call(s32[1,1]{1,0:T(1,128)S(6)} %copy.10.start_ref, s32[1,1]{1,0:T(1,128)S(6)} %copy.11.length_ref, s32[64]{0:T(128)} %order_hbm.1, f32[64,256]{1,0:T(8,128)} %table_hbm.1, f32[256,4096]{1,0:T(8,128)} %bitcast.6, bf16[32,4096]{1,0:T(8,128)(2,1)} %bitcast.7), custom_call_target="tpu_custom_call" | custom-call | tf_op jit(solution)/shard_map/exchange/pallas_call | solution.py:301
  49.7 2.0 %copy.12 = f32[8,32,4096]{2,1,0:T(8,128)} copy(f32[8,32,4096]{2,1,0:T(8,128)S(1)} %bitcast.4) | data formatting | bytes 8388608
  51.7 0.8 %copy.13 = f32[1,32,4096]{2,1,0:T(8,128)} copy(f32[1,32,4096]{2,1,0:T(8,128)S(1)} %bitcast.5) | data formatting | bytes 1048576

commit v4 on v3

--- a/solution.py
+++ b/solution.py
@@ -9,7 +9,8 @@
 
 ZDEV = 8
 ANGLES = 8
-CHUNKS = 8
+WIDTHS = (512,) * 8
+STORES = 8
 LAG = 2.5
 MESH = pl.DeviceIdType.MESH
 F32 = jnp.float32
@@ -43,7 +44,7 @@
 
 
 def exchange_kernel(
-    chunks, width,
+    widths,
     start_ref, length_ref, order_hbm, table_hbm, volume_hbm, measured_hbm,
     updated_ref, residual_ref,
     vol, meas, order_ref, table_ref, part, ray_in, pair_out, pair_in, sums, sums_in, back_out, back_in,
@@ -51,6 +52,8 @@
     project_weights, spread_weights, scale, back_weights,
     load_sem, send_sem, recv_sem, psend_sem, precv_sem,
 ):
+    chunks = len(widths)
+    spans = [(sum(widths[:c]), sum(widths[: c + 1])) for c in range(chunks)]
     slab = lax.axis_index("slab")
     ang = lax.axis_index("ang")
     n_slab = lax.axis_size("slab")
@@ -67,19 +70,22 @@
     y_of = [None] + [lax.rem(y + d, 4) for d in (1, 2, 3)]
     y_devs = [None] + [(slab, xl * 4 + y_of[d]) for d in (1, 2, 3)]
 
+    def columns_of(ref, c, *index):
+        begin, end = spans[c]
+        index = index + (slice(None),) * (len(ref.shape) - 1 - len(index))
+        return ref.at[index + (pl.ds(begin, end - begin),)]
+
     load_order = pltpu.make_async_copy(order_hbm, order_ref, load_sem.at[chunks + 2])
     load_order.start()
     load_table = pltpu.make_async_copy(table_hbm, table_ref, load_sem.at[chunks + 1])
     load_table.start()
     loads = [
-        pltpu.make_async_copy(volume_hbm.at[:, pl.ds(c * width, width)], vol.at[c], load_sem.at[c])
+        pltpu.make_async_copy(columns_of(volume_hbm, c), columns_of(vol, c), load_sem.at[c])
         for c in range(chunks)
     ]
-    for copy in loads:
+    for copy in loads[:2]:
         copy.start()
     load_measured = pltpu.make_async_copy(measured_hbm, meas, load_sem.at[chunks])
-    load_measured.start()
-
     barrier = pltpu.get_barrier_semaphore()
     greeted = (*y_devs[1:], pair_dev, *slab_devs)
     for device in greeted:
@@ -92,6 +98,9 @@
 
     load_order.wait()
     load_table.wait()
+    for copy in loads[2:]:
+        copy.start()
+    load_measured.start()
     for m in range(ANGLES):
         angle = (m % 2) * 4 + m // 2
         picked[pl.ds(m, 1), :] = table_ref[pl.ds(order_ref[angle], 1), :]
@@ -106,6 +115,16 @@
     blocks_high = high_part(blocks)
     ray_weights = jnp.concatenate([blocks_high, blocks - blocks_high], axis=0).astype(BF16)
 
+    def partial_sums(c):
+        loads[c].wait()
+        value = columns_of(vol, c)[...]
+        high = value.astype(BF16)
+        low = (value - high.astype(F32)).astype(BF16)
+        first = jnp.dot(ray_weights, high, preferred_element_type=F32)
+        second = jnp.dot(ray_weights[: ANGLES * ZDEV], low, preferred_element_type=F32)
+        total = first[: ANGLES * ZDEV] + first[ANGLES * ZDEV :] + second
+        columns_of(part, c)[...] = total.reshape(*part.shape[:-1], -1)
+    partial_sums(0)
     pl.semaphore_wait(barrier, len(greeted))
 
     def remote(src, dst, exchange, c, device):
@@ -133,26 +152,26 @@
     for copy in param_first:
         copy.start()
 
-    ray = [[remote(part.at[c, y_of[d]], ray_in.at[c, d - 1], RAY, c, y_devs[d]) for d in (1, 2, 3)] for c in range(chunks)]
-    pair = [remote(pair_out.at[c], pair_in.at[c], PAIR, c, pair_dev) for c in range(chunks)]
+    ray = [[remote(columns_of(part, c, y_of[d]), columns_of(ray_in, c, d - 1), RAY, c, y_devs[d]) for d in (2, 1, 3)] for c in range(chunks)]
+    pair = [remote(columns_of(pair_out, c), columns_of(pair_in, c), PAIR, c, pair_dev) for c in range(chunks)]
     to_slab = [
-        [remote(sums.at[c, xl if k == SIB else other], sums_in.at[c, BACK[k]], SLAB, c, slab_devs[k]) for k in FAR_FIRST]
+        [remote(columns_of(sums, c, xl if k == SIB else other), columns_of(sums_in, c, BACK[k]), SLAB, c, slab_devs[k]) for k in FAR_FIRST]
         for c in range(chunks)
     ]
     to_back = [
-        [remote(back_out.at[c, 1 + k], back_in.at[c, BACK[k]], BACKPROJ, c, slab_devs[k]) for k in FAR_FIRST]
+        [remote(columns_of(back_out, c, 1 + k), columns_of(back_in, c, BACK[k]), BACKPROJ, c, slab_devs[k]) for k in FAR_FIRST]
         for c in range(chunks)
     ]
-    pair2 = [remote(both_out.at[c], both_in.at[c], PAIR2, c, pair_dev) for c in range(chunks)]
-    gather = [[remote(gathered.at[c, y], gathered.at[c, y], GATHER, c, y_devs[d]) for d in (1, 2, 3)] for c in range(chunks)]
-    landing = (ray_in, pair_in, sums_in, back_in, both_in, gathered.at[:, pl.ds(0, 3)])
+    pair2 = [remote(columns_of(both_out, c), columns_of(both_in, c), PAIR2, c, pair_dev) for c in range(chunks)]
+    gather = [[remote(columns_of(gathered, c, y), columns_of(gathered, c, y), GATHER, c, y_devs[d]) for d in (2, 1, 3)] for c in range(chunks)]
+    landing = (ray_in, pair_in, sums_in, back_in, both_in, gathered)
 
     def wait_in(copies):
         for copy in copies:
             copy.wait_recv()
 
     def wait_exchange(exchange, c):
-        whole = landing[exchange].at[c]
+        whole = columns_of(landing[exchange], c, *((pl.ds(0, 3),) if exchange == GATHER else ()))
         remote(whole, whole, exchange, c, pair_dev).wait_recv()
 
     def tables():
@@ -205,62 +224,58 @@
         back_weights[...] = stack.T.astype(BF16)
 
     def ray_sums(c):
-        loads[c].wait()
-        value = vol[c]
-        high = value.astype(BF16)
-        low = (value - high.astype(F32)).astype(BF16)
-        first = jnp.dot(ray_weights, high, preferred_element_type=F32)
-        second = jnp.dot(ray_weights[: ANGLES * ZDEV], low, preferred_element_type=F32)
-        total = first[: ANGLES * ZDEV] + first[ANGLES * ZDEV :] + second
-        part[c] = total.reshape(part.shape[1:])
+        if c:
+            partial_sums(c)
         for copy in ray[c]:
             copy.start()
 
     def ray_arrived(c):
         wait_exchange(RAY, c)
-        pair_out[c] = part[c, y] + ray_in[c, 0] + ray_in[c, 1] + ray_in[c, 2]
+        arrived = columns_of(ray_in, c)[...]
+        columns_of(pair_out, c)[...] = columns_of(part, c, y)[...] + arrived[0] + arrived[1] + arrived[2]
         pair[c].start()
 
     def pair_arrived(c):
         wait_exchange(PAIR, c)
-        sums[c] = pair_out[c] + pair_in[c]
+        columns_of(sums, c)[...] = columns_of(pair_out, c)[...] + columns_of(pair_in, c)[...]
         for copy in to_slab[c]:
             copy.start()
 
     def project(c):
         wait_exchange(SLAB, c)
-        five = jnp.concatenate([sums[c, xl]] + [sums_in[c, k] for k in range(4)], axis=0)
+        five = jnp.concatenate([columns_of(sums, c, xl)[...]] + [columns_of(sums_in, c, k)[...] for k in range(4)], axis=0)
         high = high_part(five)
-        stack = jnp.concatenate([high, five - high, high, jnp.zeros((8, width), F32)], axis=0).astype(BF16)
+        stack = jnp.concatenate([high, five - high, high, jnp.zeros_like(high[:8])], axis=0).astype(BF16)
         projected = jnp.dot(project_weights[...], stack, preferred_element_type=F32)
-        here = (meas[:, c * width : (c + 1) * width].astype(F32) - projected) * scale[:, 0:1]
-        residual_ref[:, c * width : (c + 1) * width] = here
+        here = (columns_of(meas, c)[...].astype(F32) - projected) * scale[:, 0:1]
+        columns_of(residual_ref, c)[...] = here
         high = high_part(here)
         stack = jnp.concatenate([high, here - high, high, jnp.zeros_like(high)], axis=0).astype(BF16)
         spread = jnp.dot(spread_weights[...], stack, preferred_element_type=F32)
-        back_out[c] = spread[:40].reshape(back_out.shape[1:])
+        columns_of(back_out, c)[...] = spread[:40].reshape(*back_out.shape[:-1], -1)
         for copy in to_back[c]:
             copy.start()
 
     def back_arrived(c):
         wait_exchange(BACKPROJ, c)
-        both_out[c, xl] = back_out[c, 0] + back_in[c, SIB]
-        both_out[c, other] = back_in[c, ODD] + back_in[c, UP2] + back_in[c, DOWN2]
+        arrived = columns_of(back_in, c)[...]
+        columns_of(both_out, c, xl)[...] = columns_of(back_out, c, 0)[...] + arrived[SIB]
+        columns_of(both_out, c, other)[...] = arrived[ODD] + arrived[UP2] + arrived[DOWN2]
         pair2[c].start()
 
     def pair2_arrived(c):
         wait_exchange(PAIR2, c)
-        gathered[c, y] = both_out[c] + both_in[c]
+        columns_of(gathered, c, y)[...] = columns_of(both_out, c)[...] + columns_of(both_in, c)[...]
         for copy in gather[c]:
             copy.start()
 
     def gather_arrived(c):
         wait_exchange(GATHER, c)
-        value = gathered[c].reshape(ANGLES * ZDEV, width)
+        value = columns_of(gathered, c)[...].reshape(ANGLES * ZDEV, -1)
         high = high_part(value)
         stack = jnp.concatenate([high, value - high, high, jnp.zeros_like(high)], axis=0).astype(BF16)
         update = jnp.dot(back_weights[...], stack, preferred_element_type=F32)
-        updated_ref[:, c * width : (c + 1) * width] = vol[c] + update
+        columns_of(updated_ref, c)[...] = columns_of(vol, c)[...] + update
 
     stages = (ray_sums, ray_arrived, pair_arrived, project, back_arrived, pair2_arrived, gather_arrived)
     forwarded = False
@@ -272,20 +287,34 @@
             for copy in param_second:
                 copy.start()
             forwarded = True
-        if stage == 3 and not done_tables:
+        stages[stage](c)
+        if stage == 2 and not done_tables:
             load_measured.wait()
             tables()
             done_tables = True
-        if stage == 4 and not done_update:
+        if stage == 3 and not done_update:
             update_weights()
             done_update = True
-        stages[stage](c)
 
     for copy in param_first + param_second:
         copy.wait_send()
     for exchange in range(EXCHANGES):
-        sent = vol.at[:, pl.ds(0, SENT_ROWS[exchange])]
+        sent = vol.at[pl.ds(0, SENT_ROWS[exchange])]
         remote(sent, sent, exchange, 0, pair_dev).wait_send()
+
+
+def store_kernel(updated_ref, residual_ref, updated_hbm, residual_hbm, sem):
+    cells = updated_ref.shape[0]
+    step = cells // STORES
+    copies = [
+        pltpu.make_async_copy(updated_ref.at[pl.ds(k * step, step)], updated_hbm.at[pl.ds(k * step, step)], sem.at[k])
+        for k in range(STORES)
+    ]
+    copies.append(pltpu.make_async_copy(residual_ref, residual_hbm, sem.at[STORES]))
+    for copy in copies:
+        copy.start()
+    for copy in copies:
+        copy.wait()
 
 
 def body(volume, measured, foot_start, foot_len, order, ray_table):
@@ -293,13 +322,12 @@
     cells = slices * share
     rows = measured.shape[1]
     flat = volume.reshape(cells, columns)
-    chunks = CHUNKS
-    width = columns // chunks
+    chunks = len(WIDTHS)
     vmem = pltpu.VMEM
     smem = pl.BlockSpec(memory_space=pltpu.SMEM)
     hbm = pl.BlockSpec(memory_space=pltpu.HBM)
     updated, residual = pl.pallas_call(
-        functools.partial(exchange_kernel, chunks, width),
+        functools.partial(exchange_kernel, WIDTHS),
         out_shape=(
             jax.ShapeDtypeStruct((cells, columns), F32),
             jax.ShapeDtypeStruct((rows, columns), F32),
@@ -307,21 +335,21 @@
         in_specs=[smem, smem, hbm, hbm, hbm, hbm],
         out_specs=(pl.BlockSpec(memory_space=pltpu.VMEM),) * 2,
         scratch_shapes=[
-            vmem((chunks, cells, width), F32),
+            vmem((cells, columns), F32),
             vmem((rows, columns), BF16),
             pltpu.SMEM(order.shape, jnp.int32),
             vmem(ray_table.shape, F32),
-            vmem((chunks, 4, 2, ZDEV, width), F32),
-            vmem((chunks, 3, 2, ZDEV, width), F32),
-            vmem((chunks, 2, ZDEV, width), F32),
-            vmem((chunks, 2, ZDEV, width), F32),
-            vmem((chunks, 2, ZDEV, width), F32),
-            vmem((chunks, 4, ZDEV, width), F32),
-            vmem((chunks, 5, ZDEV, width), F32),
-            vmem((chunks, 4, ZDEV, width), F32),
-            vmem((chunks, 2, ZDEV, width), F32),
-            vmem((chunks, 2, ZDEV, width), F32),
-            vmem((chunks, 4, 2, ZDEV, width), F32),
+            vmem((4, 2, ZDEV, columns), F32),
+            vmem((3, 2, ZDEV, columns), F32),
+            vmem((2, ZDEV, columns), F32),
+            vmem((2, ZDEV, columns), F32),
+            vmem((2, ZDEV, columns), F32),
+            vmem((4, ZDEV, columns), F32),
+            vmem((5, ZDEV, columns), F32),
+            vmem((4, ZDEV, columns), F32),
+            vmem((2, ZDEV, columns), F32),
+            vmem((2, ZDEV, columns), F32),
+            vmem((4, 2, ZDEV, columns), F32),
             vmem((4, 2, 2, 8, 128), F32),
             vmem((4, 2, 8, 128), F32),
             vmem((ANGLES * ZDEV, cells), F32),
@@ -346,6 +374,19 @@
             for a in (order, ray_table, flat, measured.reshape(rows, columns))
         )
     )
+    whole = pl.BlockSpec(memory_space=pltpu.VMEM)
+    updated, residual = pl.pallas_call(
+        store_kernel,
+        out_shape=(
+            jax.ShapeDtypeStruct((cells, columns), F32),
+            jax.ShapeDtypeStruct((rows, columns), F32),
+        ),
+        in_specs=[whole, whole],
+        out_specs=(hbm, hbm),
+        scratch_shapes=[pltpu.SemaphoreType.DMA((STORES + 1,))],
+        compiler_params=pltpu.CompilerParams(vmem_limit_bytes=1024 * 1024),
+        name="store",
+    )(updated, residual)
     return (updated.reshape(slices, share, columns), residual.reshape(measured.shape))
 
 

time: 53.4 us -> 51.7 us (0.968)
  local copies, waits for them, and re-layouts: 2.81 us -> 0 us
  Pallas kernels: 47.8 us -> 49 us
    unnamed x2 -> x0, local copies, waits for them, and re-layouts: 2.81 us -> none
    pallas_call x1 -> x2, Pallas kernels: 47.8 us -> 49 us  [the longest x1 46.8 us: body(): pl.pallas_call(functools.partial(exchange_kernel, WIDTHS), out_shape=(jax...]
where the time goes in v4:
time: 51.7 us; the launch traced here: 50.9 us
  Pallas kernels  49 us (95%)
  between operations  1.93 us (4%)
    pallas_call x1, Pallas kernels, body(): pl.pallas_call(functools.partial(exchange_kernel, WIDTHS), out_shape=(jax...  46.8 us
    pallas_call x1, Pallas kernels, body(): pl.pallas_call(store_kernel, out_shape=(jax.ShapeDtypeStruct((cells, colu...  2.25 us

profile of v4, /device:TPU:2, one launch (start us, length us, event | category | flops | bytes accessed | tf_op | source)
XLA Modules:
  0.0 50.9 jit_solution(1652491368388347172)
XLA Ops:
  1.9 46.8 %exchange.1 = (f32[256,4096]{1,0:T(8,128)S(1)}, f32[32,4096]{1,0:T(8,128)S(1)}) custom-call(s32[1,1]{1,0:T(1,128)S(6)} %copy.8.start_ref, s32[1,1]{1,0:T(1,128)S(6)} %copy.9.length_ref, s32[64]{0:T(128)} %order_hbm.1, f32[64,256]{1,0:T(8,128)} %table_hbm.1, f32[256,4096]{1,0:T(8,128)} %bitcast.4, bf16[32,4096]{1,0:T(8,128)(2,1)} %bitcast.5), custom_call_target="tpu_custom_call" | custom-call | tf_op jit(solution)/shard_map/exchange/pallas_call | solution.py:329
  48.7 2.3 %store.1 = (f32[256,4096]{1,0:T(8,128)}, f32[32,4096]{1,0:T(8,128)}) custom-call(f32[256,4096]{1,0:T(8,128)S(1)} %get-tuple-element.6.updated_ref, f32[32,4096]{1,0:T(8,128)S(1)} %get-tuple-element.7.residual_ref), custom_call_target="tpu_custom_call" | custom-call | tf_op jit(solution)/shard_map/store/pallas_call | solution.py:378

commit v5 on v4

--- a/solution.py
+++ b/solution.py
@@ -75,6 +75,11 @@
         index = index + (slice(None),) * (len(ref.shape) - 1 - len(index))
         return ref.at[index + (pl.ds(begin, end - begin),)]
 
+    barrier = pltpu.get_barrier_semaphore()
+    greeted = (*y_devs[1:], pair_dev, *slab_devs)
+    for device in greeted:
+        pl.semaphore_signal(barrier, inc=1, device_id=device, device_id_type=MESH)
+
     load_order = pltpu.make_async_copy(order_hbm, order_ref, load_sem.at[chunks + 2])
     load_order.start()
     load_table = pltpu.make_async_copy(table_hbm, table_ref, load_sem.at[chunks + 1])
@@ -86,11 +91,6 @@
     for copy in loads[:2]:
         copy.start()
     load_measured = pltpu.make_async_copy(measured_hbm, meas, load_sem.at[chunks])
-    barrier = pltpu.get_barrier_semaphore()
-    greeted = (*y_devs[1:], pair_dev, *slab_devs)
-    for device in greeted:
-        pl.semaphore_signal(barrier, inc=1, device_id=device, device_id_type=MESH)
-
     first_here = jnp.full((8, 128), start_ref[0, 0], jnp.int32).astype(F32)
     length_here = jnp.full((8, 128), length_ref[0, 0], jnp.int32).astype(F32)
     params[y, xl, 0] = first_here
@@ -106,8 +106,13 @@
         picked[pl.ds(m, 1), :] = table_ref[pl.ds(order_ref[angle], 1), :]
     cells = picked.shape[1]
     share = cells // 8
-    pick = (iota((cells, cells), 0) == ang * share + lax.rem(iota((cells, cells), 1), share)).astype(F32)
-    mine = jnp.dot(picked[...], pick, precision=lax.Precision.HIGHEST, preferred_element_type=F32)
+    pick = (iota((cells, cells), 0) == ang * share + lax.rem(iota((cells, cells), 1), share)).astype(BF16)
+    chosen = picked[...]
+    high = high_part(chosen)
+    middle = high_part(chosen - high)
+    parts = jnp.concatenate([high, middle, chosen - high - middle, jnp.zeros_like(high)], axis=0).astype(BF16)
+    parts = jnp.dot(parts, pick, preferred_element_type=F32)
+    mine = parts[:ANGLES] + parts[ANGLES : 2 * ANGLES] + parts[2 * ANGLES : 3 * ANGLES]
     blocks = jnp.broadcast_to(mine[:, None, :], (ANGLES, ZDEV, cells)).reshape(ANGLES * ZDEV, cells)
     own_slice = lax.rem(iota(blocks.shape, 0), ZDEV) == iota(blocks.shape, 1) // share
     blocks = jnp.where(own_slice, blocks, 0.0)

time: 51.7 us -> 51.6 us (level)
  no operation moved by 1% of the time
where the time goes in v5:
time: 51.6 us; the launch traced here: 50.9 us
  Pallas kernels  48.9 us (95%)
  between operations  1.93 us (4%)
    pallas_call x1, Pallas kernels, body(): pl.pallas_call(functools.partial(exchange_kernel, WIDTHS), out_shape=(jax...  46.7 us
    pallas_call x1, Pallas kernels, body(): pl.pallas_call(store_kernel, out_shape=(jax.ShapeDtypeStruct((cells, colu...  2.25 us

profile of v5, /device:TPU:2, one launch (start us, length us, event | category | flops | bytes accessed | tf_op | source)
XLA Modules:
  0.0 50.9 jit_solution(730666464266878065)
XLA Ops:
  1.9 46.7 %exchange.1 = (f32[256,4096]{1,0:T(8,128)S(1)}, f32[32,4096]{1,0:T(8,128)S(1)}) custom-call(s32[1,1]{1,0:T(1,128)S(6)} %copy.8.start_ref, s32[1,1]{1,0:T(1,128)S(6)} %copy.9.length_ref, s32[64]{0:T(128)} %order_hbm.1, f32[64,256]{1,0:T(8,128)} %table_hbm.1, f32[256,4096]{1,0:T(8,128)} %bitcast.4, bf16[32,4096]{1,0:T(8,128)(2,1)} %bitcast.5), custom_call_target="tpu_custom_call" | custom-call | tf_op jit(solution)/shard_map/exchange/pallas_call | solution.py:334
  48.6 2.3 %store.1 = (f32[256,4096]{1,0:T(8,128)}, f32[32,4096]{1,0:T(8,128)}) custom-call(f32[256,4096]{1,0:T(8,128)S(1)} %get-tuple-element.6.updated_ref, f32[32,4096]{1,0:T(8,128)S(1)} %get-tuple-element.7.residual_ref), custom_call_target="tpu_custom_call" | custom-call | tf_op jit(solution)/shard_map/store/pallas_call | solution.py:383
